TPU v7x, 32 devices: a whole 2x2x4 slice. The times are simulated.
32 devices in a mesh: ga: 8 (over z, x), band: 4 (over y, core).
Axes of the slice: x: 2, y: 2, z: 4, core: 2. Of those that a mesh axis runs over, the one named last changes fastest.
Arguments:
- coeffs: bfloat16 [2, 512, 40960], P(None, ('ga', 'band')), may hold values from -6 to 6
- projectors: bfloat16 [1280, 2, 40960], P(None, None, 'ga'), may hold values from -0.01953125 to 0.01953125
- block_coupling: float32 [1280, 18], replicated, may hold values from -12 to 12
- atom_counts: int32 [160], replicated, may hold values from 4 to 18, as said below
- wave_counts: int32 [8], P('ga'), may hold values from 3840 to 5120
Outputs:
- applied: bfloat16 [2, 512, 40960], P(None, ('ga', 'band'))
- band_energy: float32 [512], P(('ga', 'band'))
- total_energy: float32 [], replicated
Inputs may be any that keep to these rules, and one draw needn't show every extreme that they name: `atom_counts`: each atom has 4, 8 or 18 projectors, the counts sum to 1280 and the largest is 18.
All inputs are finite; a program needn't handle non-finite values.
Results may differ from a plain program's by a relative error of at most 0.013.
Values may be sent and summed in bfloat16 or wider, within the bound.
No kernel may reach another device: no remote copies, remote signals or barrier semaphores. Data moves between devices by JAX's collectives and lax.ppermute only.
A program may use at most 128 MiB of HBM per device.

v0:
```python
import math

import jax
import jax.numpy as jnp
from jax import lax
from jax.sharding import PartitionSpec as P


def block_tables(atom_counts, row_ids):
    atom_ends = jnp.cumsum(atom_counts)
    atom_starts = atom_ends - atom_counts
    inside = (atom_starts[None, :] <= row_ids[:, None]) & (atom_ends[None, :] > row_ids[:, None])
    block_first = jnp.sum(jnp.where(inside, atom_starts[None, :], 0), axis=1)
    block_length = jnp.sum(jnp.where(inside, atom_counts[None, :], 0), axis=1)
    return (block_first, block_length)


def coupling_matrix(block_first, block_length, coupling_rows, column_count):
    column_ids = lax.iota(jnp.int32, column_count)
    offsets = column_ids[None, :] - block_first[:, None]
    matrix = jnp.zeros((coupling_rows.shape[0], column_count), jnp.float32)
    for offset in range(coupling_rows.shape[1]):
        hit = (offsets == offset) & (offset < block_length[:, None])
        matrix = jnp.where(hit, coupling_rows[:, offset : offset + 1], matrix)
    return matrix


def shards(coeffs, projectors, block_coupling, atom_counts, wave_counts):
    moved_bands = lax.all_to_all(coeffs, "ga", split_axis=2, concat_axis=1, tiled=True)
    own_bands = coeffs.shape[1]
    group_bands = moved_bands.shape[1]
    wave_slots = projectors.shape[2]
    proj_total_rows = projectors.shape[0]
    in_sphere = (lax.iota(jnp.int32, wave_slots) < wave_counts[0]).astype(jnp.float32)
    masked = moved_bands * in_sphere.astype(jnp.bfloat16)
    real_part = masked[0]
    imag_part = masked[1]
    stacked = jnp.concatenate(
        [jnp.concatenate([real_part, imag_part], 1), jnp.concatenate([imag_part, -real_part], 1)], 0
    )
    flat_beta = projectors.reshape(proj_total_rows, 2 * wave_slots)
    contract_last = (((1,), (1,)), ((), ()))
    contract_first = (((0,), (0,)), ((), ()))
    ga_index = lax.axis_index("ga")
    local_terms = lax.dot_general(
        flat_beta, stacked, contract_last, preferred_element_type=jnp.float32
    )
    projections = lax.psum(local_terms, "ga")
    block_first, block_length = block_tables(atom_counts, lax.iota(jnp.int32, proj_total_rows))
    matrix = coupling_matrix(block_first, block_length, block_coupling, proj_total_rows)
    coupled = jnp.dot(
        matrix, projections, precision=lax.Precision.HIGHEST, preferred_element_type=jnp.float32
    )
    energy_terms = jnp.sum(projections * coupled, axis=0)
    group_energy = (energy_terms[:group_bands] + energy_terms[group_bands:]) / proj_total_rows
    band_energy = lax.dynamic_slice_in_dim(group_energy, ga_index * own_bands, own_bands, 0)
    total_energy = lax.psum(jnp.sum(group_energy), "band")
    products = lax.dot_general(
        coupled.astype(jnp.bfloat16), flat_beta, contract_first, preferred_element_type=jnp.float32
    )
    band_total = own_bands * lax.axis_size("ga") * lax.axis_size("band")
    total_energy = total_energy / math.sqrt(band_total)
    real_out = products[:group_bands, :wave_slots] - products[group_bands:, wave_slots:]
    imag_out = products[:group_bands, wave_slots:] + products[group_bands:, :wave_slots]
    result = (jnp.stack([real_out, imag_out]) * in_sphere).astype(jnp.bfloat16)
    applied = lax.all_to_all(result, "ga", split_axis=1, concat_axis=2, tiled=True)
    return (applied, band_energy, total_energy)


def solution(mesh):
    placed = (P(None, ("ga", "band"), None), P(None, None, "ga"), P(), P(), P("ga"))
    return jax.shard_map(
        shards,
        mesh=mesh,
        in_specs=placed,
        out_specs=(P(None, ("ga", "band"), None), P(("ga", "band")), P()),
        check_vma=False,
    )
```

profile of v0, /device:TPU:0, one launch (start us, length us, event | category | flops | bytes accessed | tf_op | source)
XLA Modules:
  0.0 430.2 jit_solution(13984395675737779399)
XLA Ops:
  7.2 38.0 %copy.21 = bf16[2,16,40960]{1,0,2:T(2,128)(2,1)} copy(bf16[2,16,40960]{2,1,0:T(8,128)(2,1)} %param.5) | data formatting | bytes 5242880 | tf_op args[0]
  45.1 24.1 %reshape.129 = bf16[8,2,81920]{2,1,0:T(2,128)(2,1)} reshape(bf16[40960,2,16]{2,1,0:T(2,128)(2,1)} %bitcast.40) | data formatting | bytes 5242880
  69.2 7.3 %all-to-all-start = ((bf16[8,2,81920]{2,1,0:T(2,128)(2,1)}), bf16[8,2,81920]{2,1,0:T(2,128)(2,1)S(1)}, u32[]{:S(2)}, u32[]{:S(2)}) async-start(bf16[8,2,81920]{2,1,0:T(2,128)(2,1)} %reshape.129), calls=%async_computation | async-start | bytes 5242880 | tf_op jit(solution)/shard_map/all_to_all | solution.py:29
  76.5 0.2 all-reduce.3.cloned.1.call-start
  77.4 23.8 %copy.29 = bf16[160,8,2,5120]{3,1,2,0:T(8,128)(2,1)} copy(bf16[160,8,2,5120]{3,2,1,0:T(2,128)(2,1)} %bitcast.41) | data formatting | bytes 52428800
  101.1 34.8 %all-to-all-done = bf16[8,2,81920]{2,1,0:T(2,128)(2,1)S(1)} async-done(((bf16[8,2,81920]{2,1,0:T(2,128)(2,1)}), bf16[8,2,81920]{2,1,0:T(2,128)(2,1)S(1)}, u32[]{:S(2)}, u32[]{:S(2)}) %all-to-all-start) | async-done | bytes 2621472 | tf_op jit(solution)/shard_map/all_to_all | solution.py:29
  136.0 17.1 %reshape.130 = bf16[40960,2,16]{2,1,0:T(2,128)(2,1)} reshape(bf16[8,2,81920]{2,1,0:T(2,128)(2,1)S(1)} %all-to-all-done) | data formatting | bytes 5242880
  153.0 37.5 %copy.28 = bf16[2,16,8,5120]{3,1,2,0:T(8,128)(2,1)S(1)} copy(bf16[2,16,8,5120]{1,0,3,2:T(2,128)(2,1)} %bitcast.39) | data formatting | bytes 5242880 | tf_op jit(solution)/shard_map/all_to_all | solution.py:29
  190.5 0.3 bitcast_multiply_fusion
  190.9 0.2 slice_bitcast_fusion.1
  191.1 0.1 fusion.168
  191.2 28.8 %fusion.138 = f32[1280,256]{0,1:T(8,128)} fusion(bf16[1280,10240]{1,0:T(8,128)(2,1)} %bitcast.37, bf16[128,5120]{1,0:T(8,128)(2,1)S(1)} %fusion.168, bf16[128,5120]{1,0:T(8,128)(2,1)S(1)} %get-tuple-element.28, bf16[128,5120]{1,0:T(8,128)(2,1)S(1)} %get-tuple-element.27), kind=kOutput, calls=%fused_computation.122 | convolution fusion | flops 6731857920 | bytes 31457280 | tf_op jit(solution)/shard_map/dot_general | solution.py:45
  220.1 0.3 reduce-window.9
  220.4 0.1 slice.88
  220.5 0.1 slice_reduce_fusion.18
  220.6 0.2 slice_reduce_fusion.17
  220.9 0.3 select_reduce_fusion
  221.3 81.7 %all-reduce.3.cloned.1.call-done = f32[1280,256]{0,1:T(8,128)} async-done(((f32[1280,256]{0,1:T(8,128)}), f32[1280,256]{0,1:T(8,128)}) %all-reduce.3.cloned.1.call-update) | async-done | bytes 1310736 | tf_op jit(solution)/shard_map/psum | solution.py:48
  303.0 29.8 %fusion = f32[1280,256]{1,0:T(8,128)} fusion(f32[1280,256]{0,1:T(8,128)} %all-reduce.3.cloned.1.call-done, f32[1280]{0:T(1024)S(1)} %get-tuple-element.19, f32[1280]{0:T(1024)S(1)} %get-tuple-element.20, f32[1280]{0:T(1024)S(1)} %get-tuple-element.4, f32[1280]{0:T(1024)S(1)} %get-tuple-element.5, f32[1280]{0:T(1024)S(1)} %get-tuple-element.6, ...), kind=kOutput, calls=%fused_computation | convolution fusion | flops 5123276800 | bytes 2741760 | tf_op jit(solution)/shard_map/dot_general | solution.py:51
  332.7 13.0 %fusion.144 = f32[256,10240]{1,0:T(8,128)S(1)} fusion(bf16[1280,10240]{1,0:T(8,128)(2,1)} %bitcast.38, f32[1280,256]{1,0:T(8,128)} %fusion), kind=kOutput, calls=%fused_computation.136 | convolution fusion | flops 6711214080 | bytes 38010880 | tf_op jit(solution)/shard_map/dot_general | solution.py:58
  345.8 0.8 fusion.142
  346.5 0.5 fusion.81
  347.0 4.2 copy.24
  351.2 3.7 all-to-all-start.1
  354.9 2.8 copy.26
  357.6 1.9 multiply_reduce_fusion
  359.5 0.6 fusion.169
  360.2 7.3 %psum.15 = f32[]{:T(128)} all-reduce(f32[]{:T(128)} %get-tuple-element.23), channel_id=1, replica_groups=mesh['ga'=8,'band'=4] {'band'}, use_global_device_ids=true, to_apply=%region_7.8 | all-reduce | flops 1 | bytes 8 | tf_op jit(solution)/shard_map/psum | solution.py:57
  367.5 0.6 dynamic_slice.3
  368.7 45.7 %all-to-all-done.1 = bf16[2,128,5120]{2,0,1:T(2,128)(2,1)S(1)} async-done(((bf16[2,128,5120]{2,0,1:T(2,128)(2,1)}), bf16[2,128,5120]{2,0,1:T(2,128)(2,1)S(1)}, u32[]{:S(2)}, u32[]{:S(2)}) %all-to-all-start.1) | async-done | bytes 2621472 | tf_op jit(solution)/shard_map/all_to_all | solution.py:66
  414.4 2.9 copy.25
  417.3 4.5 %all_to_all.33 = bf16[2,16,40960]{2,1,0:T(8,128)(2,1)} reshape(bf16[2,16,8,5120]{3,2,1,0:T(8,128)(2,1)} %copy.25) | data formatting | bytes 5242880 | tf_op jit(solution)/shard_map/all_to_all | solution.py:66
  (11 shorter events, 0.2 us)
Async XLA Ops:
  69.2 66.8 %all-to-all-start = ((bf16[8,2,81920]{2,1,0:T(2,128)(2,1)}), bf16[8,2,81920]{2,1,0:T(2,128)(2,1)S(1)}, u32[]{:S(2)}, u32[]{:S(2)}) async-start(bf16[8,2,81920]{2,1,0:T(2,128)(2,1)} %reshape.129), calls=%async_computation | async-start | bytes 5242880 | tf_op jit(solution)/shard_map/all_to_all | solution.py:29
  76.5 226.5 %all-reduce.3.cloned.1.call-start = ((), (), s32[]{:S(2)}) async-start(), calls=%async_computation.2 | async-start | bytes 2621440 | tf_op jit(solution)/shard_map/psum | solution.py:48
  191.2 28.9 %copy-start.1 = (s32[160]{0:T(256)S(1)}, s32[160]{0:T(256)}, u32[]{:S(2)}) copy-start(s32[160]{0:T(256)} %param.8) | copy-start | bytes 1924
  191.2 29.4 %copy-start = (f32[1280,18]{0,1:T(8,128)S(1)}, f32[1280,18]{0,1:T(8,128)}, u32[]{:S(2)}) copy-start(f32[1280,18]{0,1:T(8,128)} %param.7) | copy-start | bytes 276484
  351.2 63.2 %all-to-all-start.1 = ((bf16[2,128,5120]{2,0,1:T(2,128)(2,1)}), bf16[2,128,5120]{2,0,1:T(2,128)(2,1)S(1)}, u32[]{:S(2)}, u32[]{:S(2)}) async-start(bf16[2,128,5120]{2,0,1:T(2,128)(2,1)} %copy.24), calls=%async_computation.1 | async-start | bytes 5242880 | tf_op jit(solution)/shard_map/all_to_all | solution.py:66
Sparse Core Ops, SparseCore 0:
  220.2 82.7 all-reduce.2
where the time goes:
time: 438 us; the launch traced here: 430 us
  waiting for transfers between devices  162 us (37%)
  local copies, waits for them, and re-layouts  156 us (36%)
  matrix products  71.6 us (16%)
  between operations  17 us (4%)
  starting transfers between devices  11.2 us (3%)
  blocking collectives  7.34 us (2%)
  other arithmetic  4.94 us (1%)
    unnamed x8, local copies, waits for them, and re-layouts  103 us
    psum x1, waiting for transfers between devices, shards(): projections = lax.psum(local_terms, 'ga')  81.7 us
    all_to_all x1, waiting for transfers between devices, shards(): lax.all_to_all(result, 'ga', split_axis=1, concat_axis=2, tiled=True)  45.7 us
    all_to_all x1, local copies, waits for them, and re-layouts, shards(): lax.all_to_all(coeffs, 'ga', split_axis=2, concat_axis=1, tiled=True)  37.5 us
    all_to_all x1, waiting for transfers between devices, shards(): lax.all_to_all(coeffs, 'ga', split_axis=2, concat_axis=1, tiled=True)  34.8 us
    dot_general x1, matrix products, shards(): jnp.dot(matrix, projections, precision=lax.Precision.HIGHEST, preferred_e...  29.8 us
    dot_general x1, matrix products, shards(): lax.dot_general(flat_beta, stacked, contract_last, preferred_element_type...  28.8 us
    dot_general x1, matrix products, shards(): lax.dot_general(coupled.astype(jnp.bfloat16), flat_beta, contract_first,...  13 us
  transfers between devices with their start and end apart: 3, of which 3 were waited for; matrix products, arithmetic and copies ran while one was open for 7% of the time, Pallas kernels for 0%

commit v1 on v0

v1 whole, which is shorter than its diff:
```python
import math

import jax
import jax.numpy as jnp
from jax import lax
from jax.experimental import pallas as pl
from jax.experimental.pallas import tpu as pltpu
from jax.sharding import PartitionSpec as P


def block_tables(atom_counts, row_ids):
    atom_ends = jnp.cumsum(atom_counts)
    atom_starts = atom_ends - atom_counts
    inside = (atom_starts[None, :] <= row_ids[:, None]) & (atom_ends[None, :] > row_ids[:, None])
    block_first = jnp.sum(jnp.where(inside, atom_starts[None, :], 0), axis=1)
    block_length = jnp.sum(jnp.where(inside, atom_counts[None, :], 0), axis=1)
    return (block_first, block_length)


def shift_weights(block_first, block_length, coupling):
    rows, most = coupling.shape
    columns = coupling.T
    shifts = lax.iota(jnp.int32, 2 * most - 1) - (most - 1)
    place = shifts[:, None] + (lax.iota(jnp.int32, rows) - block_first)[None, :]
    weights = jnp.zeros(place.shape, jnp.float32)
    for k in range(most):
        hit = (place == k) & (k < block_length)[None, :]
        weights = jnp.where(hit, columns[k][None, :], weights)
    return weights


def project(moved, beta, wave_counts, tile):
    sources, _, bands, slots = moved.shape
    rows = sources * 2 * bands
    count = beta.shape[1]

    def kernel(counts_ref, x_ref, beta_ref, out_ref, masked_ref):
        @pl.when(pl.program_id(0) == 0)
        def _():
            inside = lax.broadcasted_iota(jnp.int32, (2 * bands, slots), 1) < counts_ref[0]
            for s in range(sources):
                part = x_ref[s].reshape(2 * bands, slots)
                masked_ref[s * 2 * bands : (s + 1) * 2 * bands, :] = jnp.where(inside, part, jnp.zeros_like(part))

        nt = (((1,), (1,)), ((), ()))
        masked = masked_ref[...]
        first = lax.dot_general(masked, beta_ref[0], nt, preferred_element_type=jnp.float32)
        second = lax.dot_general(masked, beta_ref[1], nt, preferred_element_type=jnp.float32)
        for s in range(sources):
            re = slice(s * 2 * bands, s * 2 * bands + bands)
            im = slice(s * 2 * bands + bands, (s + 1) * 2 * bands)
            out_ref[s, :bands, :] = first[re] + second[im]
            out_ref[s, bands:, :] = first[im] - second[re]

    return pl.pallas_call(
        kernel,
        grid_spec=pltpu.PrefetchScalarGridSpec(
            num_scalar_prefetch=1,
            grid=(count // tile,),
            in_specs=[
                pl.BlockSpec((sources, 2, bands, slots), lambda i, c: (0, 0, 0, 0)),
                pl.BlockSpec((2, tile, slots), lambda i, c: (0, i, 0)),
            ],
            out_specs=pl.BlockSpec((sources, 2 * bands, tile), lambda i, c: (0, 0, i)),
            scratch_shapes=[pltpu.VMEM((rows, slots), jnp.bfloat16)],
        ),
        out_shape=jax.ShapeDtypeStruct((sources, 2 * bands, count), jnp.float32),
        name="project",
    )(wave_counts, moved, beta)


def couple(parts, weights):
    sources, rows, count = parts.shape
    shifts = weights.shape[0]
    bands = rows // 2
    most = (shifts + 1) // 2

    def kernel(parts_ref, weights_ref, low_ref, energy_ref):
        total = parts_ref[0]
        for s in range(1, sources):
            total = total + parts_ref[s]
        summed = jnp.zeros_like(total)
        for k in range(shifts):
            amount = (most - 1 - k) % count
            moved = total if amount == 0 else pltpu.roll(total, amount, 1)
            summed = summed + weights_ref[k : k + 1, :] * moved
        low_ref[...] = summed.astype(jnp.bfloat16)
        terms = total * summed
        energy = jnp.sum(terms[:bands] + terms[bands:], axis=1, keepdims=True)
        energy_ref[...] = jnp.broadcast_to(energy, energy_ref.shape)

    return pl.pallas_call(
        kernel,
        out_shape=(
            jax.ShapeDtypeStruct((rows, count), jnp.bfloat16),
            jax.ShapeDtypeStruct((bands, 128), jnp.float32),
        ),
        name="couple",
    )(parts, weights)


def apply(coupled, beta, wave_counts, tile):
    sources, rows, count = coupled.shape
    bands = rows // 2
    slots = beta.shape[2]

    def kernel(counts_ref, c_ref, beta_ref, out_ref):
        at = pl.program_id(0) * tile
        inside = lax.broadcasted_iota(jnp.int32, (bands, tile), 1) + at < counts_ref[0]
        left = c_ref[...].reshape(sources * rows, count)
        nn = (((1,), (0,)), ((), ()))
        first = lax.dot_general(left, beta_ref[0], nn, preferred_element_type=jnp.float32)
        second = lax.dot_general(left, beta_ref[1], nn, preferred_element_type=jnp.float32)
        for s in range(sources):
            re = slice(s * rows, s * rows + bands)
            im = slice(s * rows + bands, (s + 1) * rows)
            out_ref[s, 0] = jnp.where(inside, first[re] - second[im], 0.0).astype(jnp.bfloat16)
            out_ref[s, 1] = jnp.where(inside, first[im] + second[re], 0.0).astype(jnp.bfloat16)

    return pl.pallas_call(
        kernel,
        grid_spec=pltpu.PrefetchScalarGridSpec(
            num_scalar_prefetch=1,
            grid=(slots // tile,),
            in_specs=[
                pl.BlockSpec((sources, rows, count), lambda i, c: (0, 0, 0)),
                pl.BlockSpec((2, count, tile), lambda i, c: (0, 0, i)),
            ],
            out_specs=pl.BlockSpec((sources, 2, bands, tile), lambda i, c: (0, 0, 0, i)),
        ),
        out_shape=jax.ShapeDtypeStruct((sources, 2, bands, slots), jnp.bfloat16),
        name="apply",
    )(wave_counts, coupled, beta)


def shards(coeffs, projectors, block_coupling, atom_counts, wave_counts):
    own_bands = coeffs.shape[1]
    ga = lax.axis_size("ga")
    slots = projectors.shape[2]
    count = projectors.shape[0]
    sent = coeffs.reshape(2, own_bands, ga, slots).transpose(2, 0, 1, 3)
    moved = lax.all_to_all(sent, "ga", split_axis=0, concat_axis=0, tiled=True)
    beta = projectors.transpose(1, 0, 2)
    block_first, block_length = block_tables(atom_counts, lax.iota(jnp.int32, count))
    weights = shift_weights(block_first, block_length, block_coupling)
    partial = project(moved, beta, wave_counts, 256)
    parts = lax.all_to_all(partial, "ga", split_axis=0, concat_axis=0, tiled=True)
    low, energy = couple(parts, weights)
    band_energy = energy[:, 0] / count
    band_total = own_bands * ga * lax.axis_size("band")
    total_energy = lax.psum(jnp.sum(band_energy), ("ga", "band")) / math.sqrt(band_total)
    coupled = lax.all_gather(low, "ga", axis=0)
    result = apply(coupled, beta, wave_counts, 512)
    back = lax.all_to_all(result, "ga", split_axis=0, concat_axis=0, tiled=True)
    applied = back.transpose(1, 2, 0, 3).reshape(2, own_bands, ga * slots)
    return (applied, band_energy, total_energy)


def solution(mesh):
    placed = (P(None, ("ga", "band"), None), P(None, None, "ga"), P(), P(), P("ga"))
    return jax.shard_map(
        shards,
        mesh=mesh,
        in_specs=placed,
        out_specs=(P(None, ("ga", "band"), None), P(("ga", "band")), P()),
        check_vma=False,
    )
```

time: 438 us -> 259 us (0.59); the launches traced: 430 us -> 258 us
  local copies, waits for them, and re-layouts: 156 us -> 31.9 us
  blocking collectives: 7.34 us -> 108 us
  waiting for transfers between devices: 162 us -> 63.9 us
  matrix products: 71.6 us -> 0 us
  Pallas kernels: 0 us -> 33.6 us
  between operations: 17 us -> 3.14 us
    psum x1 -> x0, waiting for transfers between devices: 81.7 us -> none  [shards(): projections = lax.psum(local_terms, 'ga')]
    unnamed x8 -> x11, local copies, waits for them, and re-layouts: 103 us -> 26.3 us
    dot_general x3 -> x0, matrix products: 71.6 us -> none  [the longest x1 29.8 us: shards(): jnp.dot(matrix, projections, precision=lax.Precision.HIGHEST, preferred_e...]
    psum x1, blocking collectives: 7.34 us -> 73.5 us  [shards(): lax.psum(jnp.sum(band_energy), ('ga', 'band')) / math.sqrt(band_total)]
    all_to_all x3 -> x0, local copies, waits for them, and re-layouts: 44.9 us -> none  [the longest x1 37.5 us: shards(): lax.all_to_all(coeffs, 'ga', split_axis=2, concat_axis=1, tiled=True)]
    all_gather x0 -> x1, blocking collectives: none -> 34.2 us  [shards(): coupled = lax.all_gather(low, 'ga', axis=0)]
    pallas_call x0 -> x3, Pallas kernels: none -> 33.6 us  [the longest x1 15.8 us: apply(): pl.pallas_call(kernel, grid_spec=pltpu.PrefetchScalarGridSpec(num_scalar_...]
    all_to_all x2 -> x3, waiting for transfers between devices: 80.5 us -> 63.9 us  [the longest x1 35 us: shards(): moved = lax.all_to_all(sent, 'ga', split_axis=0, concat_axis=0, tiled=True)]
  transfers between devices with their start and end apart: 3 -> 3, of which waited for: 3 -> 2; matrix products, arithmetic and copies ran while one was open for 7% -> 11% of each run, Pallas kernels for 0% -> 0%
where the time goes in v1:
time: 259 us; the launch traced here: 258 us
  blocking collectives  108 us (42%)
  waiting for transfers between devices  63.9 us (25%)
  Pallas kernels  33.6 us (13%)
  local copies, waits for them, and re-layouts  31.9 us (12%)
  starting transfers between devices  14.8 us (6%)
  between operations  3.14 us (1%)
  other arithmetic  2.87 us (1%)
    psum x1, blocking collectives, shards(): lax.psum(jnp.sum(band_energy), ('ga', 'band')) / math.sqrt(band_total)  73.5 us
    all_to_all x1, waiting for transfers between devices, shards(): moved = lax.all_to_all(sent, 'ga', split_axis=0, concat_axis=0, tiled=True)  35 us
    all_gather x1, blocking collectives, shards(): coupled = lax.all_gather(low, 'ga', axis=0)  34.2 us
    all_to_all x1, waiting for transfers between devices, shards(): lax.all_to_all(partial, 'ga', split_axis=0, concat_axis=0, tiled=True)  28.8 us
    unnamed x11, local copies, waits for them, and re-layouts  26.3 us
    pallas_call x1, Pallas kernels, apply(): pl.pallas_call(kernel, grid_spec=pltpu.PrefetchScalarGridSpec(num_scalar_...  15.8 us
    pallas_call x1, Pallas kernels, project(): pl.pallas_call(kernel, grid_spec=pltpu.PrefetchScalarGridSpec(num_scalar_...  14.2 us
    all_to_all x1, starting transfers between devices, shards(): moved = lax.all_to_all(sent, 'ga', split_axis=0, concat_axis=0, tiled=True)  7.28 us
  transfers between devices with their start and end apart: 3, of which 2 were waited for; matrix products, arithmetic and copies ran while one was open for 11% of the time, Pallas kernels for 0%

profile of v1, /device:TPU:0, one launch (start us, length us, event | category | flops | bytes accessed | tf_op | source)
XLA Modules:
  0.0 257.9 jit_solution(645230936117285768)
XLA Ops:
  0.6 3.4 %copy.20 = bf16[2,2,8,8,5120]{4,3,1,0,2:T(8,128)(2,1)} copy(bf16[2,2,8,8,5120]{4,3,2,1,0:T(8,128)(2,1)} %bitcast.22) | data formatting | bytes 5242880 | tf_op jit(solution)/shard_map/reshape | solution.py:141
  4.1 7.3 %all-to-all-start = ((bf16[8,2,16,5120]{3,2,1,0:T(8,128)(2,1)}), bf16[8,2,16,5120]{3,2,1,0:T(8,128)(2,1)S(1)}, u32[]{:S(2)}, u32[]{:S(2)}) async-start(bf16[8,2,16,5120]{3,2,1,0:T(8,128)(2,1)} %bitcast.18), calls=%async_computation | async-start | bytes 5242880 | tf_op jit(solution)/shard_map/all_to_all | solution.py:142
  12.0 23.8 %copy.19 = bf16[1280,2,5120]{2,0,1:T(8,128)(2,1)} copy(bf16[1280,2,5120]{2,1,0:T(2,128)(2,1)} %param.6) | data formatting | bytes 52428800 | tf_op args[1]
  35.8 35.0 %all-to-all-done.x_ref = bf16[8,2,16,5120]{3,2,1,0:T(8,128)(2,1)S(1)} async-done(((bf16[8,2,16,5120]{3,2,1,0:T(8,128)(2,1)}), bf16[8,2,16,5120]{3,2,1,0:T(8,128)(2,1)S(1)}, u32[]{:S(2)}, u32[]{:S(2)}) %all-to-all-start) | async-done | bytes 2621472 | tf_op jit(solution)/shard_map/all_to_all | solution.py:142
  70.8 0.0 copy-start
  70.8 1.5 copy-done
  72.3 14.2 %project.1 = f32[8,32,1280]{2,1,0:T(8,128)} custom-call(s32[1]{0:T(128)S(6)} %copy.21.counts_ref, bf16[8,2,16,5120]{3,2,1,0:T(8,128)(2,1)} %copy-done, bf16[2,1280,5120]{2,1,0:T(8,128)(2,1)} %bitcast.19), custom_call_target="tpu_custom_call" | custom-call | tf_op jit(solution)/shard_map/project/pallas_call | solution.py:55
  86.5 0.0 copy-start.3
  86.5 0.0 copy-start.2
  86.5 3.8 %all-to-all-start.1 = ((f32[8,32,1280]{2,1,0:T(8,128)}), f32[8,32,1280]{2,1,0:T(8,128)S(1)}, u32[]{:S(2)}, u32[]{:S(2)}) async-start(f32[8,32,1280]{2,1,0:T(8,128)} %project.1), calls=%async_computation.1 | async-start | bytes 2621440 | tf_op jit(solution)/shard_map/all_to_all | solution.py:147
  90.3 0.0 copy-done.3
  90.3 0.3 reduce-window.9
  90.6 0.1 slice.67
  90.8 0.1 slice_reduce_fusion.18
  90.9 0.0 copy-done.2
  90.9 0.2 slice_reduce_fusion.17
  91.1 0.1 add_bitcast_fusion
  91.2 0.3 select_reduce_fusion
  91.6 1.5 select_select_fusion.weights_ref
  93.0 28.8 %all-to-all-done.1.parts_ref = f32[8,32,1280]{2,1,0:T(8,128)S(1)} async-done(((f32[8,32,1280]{2,1,0:T(8,128)}), f32[8,32,1280]{2,1,0:T(8,128)S(1)}, u32[]{:S(2)}, u32[]{:S(2)}) %all-to-all-start.1) | async-done | bytes 1310752 | tf_op jit(solution)/shard_map/all_to_all | solution.py:147
  121.9 0.0 copy-start.1
  121.9 1.1 copy-done.1
  122.9 3.5 %couple.1 = (bf16[32,1280]{1,0:T(8,128)(2,1)}, f32[16,128]{1,0:T(8,128)}) custom-call(f32[8,32,1280]{2,1,0:T(8,128)} %copy-done.1, f32[35,1280]{1,0:T(8,128)} %select_select_fusion.weights_ref), custom_call_target="tpu_custom_call" | custom-call | tf_op jit(solution)/shard_map/couple/pallas_call | solution.py:92
  126.5 34.2 %all-gather = bf16[256,1280]{1,0:T(8,128)(2,1)} all-gather(bf16[32,1280]{1,0:T(8,128)(2,1)} %get-tuple-element.5), channel_id=2, replica_groups=mesh['ga'=8,'band'=4] {'ga'}, dimensions={0}, use_global_device_ids=true | all-gather | bytes 737280 | tf_op jit(solution)/shard_map/all_gather | solution.py:152
  160.7 15.8 %apply.1 = bf16[8,2,16,5120]{3,2,1,0:T(8,128)(2,1)} custom-call(s32[1]{0:T(128)S(6)} %copy.21.counts_ref, bf16[8,32,1280]{2,1,0:T(8,128)(2,1)} %bitcast.24, bf16[2,1280,5120]{2,1,0:T(8,128)(2,1)} %bitcast.20), custom_call_target="tpu_custom_call" | custom-call | tf_op jit(solution)/shard_map/apply/pallas_call | solution.py:120
  176.5 0.0 copy-start.4
  176.5 3.8 %all-to-all-start.2 = ((bf16[8,2,16,5120]{3,2,1,0:T(8,128)(2,1)}), bf16[8,2,16,5120]{3,2,1,0:T(8,128)(2,1)S(1)}, u32[]{:S(2)}, u32[]{:S(2)}) async-start(bf16[8,2,16,5120]{3,2,1,0:T(8,128)(2,1)} %apply.1), calls=%async_computation.2 | async-start | bytes 5242880 | tf_op jit(solution)/shard_map/all_to_all | solution.py:154
  180.3 0.0 copy-done.4
  180.3 0.6 fusion.19
  180.9 73.5 %psum.7 = f32[]{:T(128)} all-reduce(f32[]{:T(128)} %get-tuple-element.25), channel_id=1, replica_groups=mesh['ga'=8,'band'=4] {'ga','band'}, use_global_device_ids=true, to_apply=%region_5.6 | all-reduce | flops 1 | bytes 8 | tf_op jit(solution)/shard_map/psum | solution.py:151
  255.0 0.0 all-to-all-done.2
  255.1 1.7 copy.16
  (6 shorter events, 0.1 us)
Async XLA Ops:
  4.1 66.8 %all-to-all-start = ((bf16[8,2,16,5120]{3,2,1,0:T(8,128)(2,1)}), bf16[8,2,16,5120]{3,2,1,0:T(8,128)(2,1)S(1)}, u32[]{:S(2)}, u32[]{:S(2)}) async-start(bf16[8,2,16,5120]{3,2,1,0:T(8,128)(2,1)} %bitcast.18), calls=%async_computation | async-start | bytes 5242880 | tf_op jit(solution)/shard_map/all_to_all | solution.py:142
  70.8 1.5 copy-start
  86.5 3.8 %copy-start.3 = (s32[160]{0:T(256)S(1)}, s32[160]{0:T(256)}, u32[]{:S(2)}) copy-start(s32[160]{0:T(256)} %param.8) | copy-start | bytes 1924
  86.5 4.3 %copy-start.2 = (f32[1280,18]{0,1:T(8,128)S(1)}, f32[1280,18]{0,1:T(8,128)}, u32[]{:S(2)}) copy-start(f32[1280,18]{0,1:T(8,128)} %param.7) | copy-start | bytes 276484
  86.5 35.3 %all-to-all-start.1 = ((f32[8,32,1280]{2,1,0:T(8,128)}), f32[8,32,1280]{2,1,0:T(8,128)S(1)}, u32[]{:S(2)}, u32[]{:S(2)}) async-start(f32[8,32,1280]{2,1,0:T(8,128)} %project.1), calls=%async_computation.1 | async-start | bytes 2621440 | tf_op jit(solution)/shard_map/all_to_all | solution.py:147
  121.9 1.1 copy-start.1
  176.5 3.8 %copy-start.4 = (f32[16,128]{1,0:T(8,128)S(1)}, f32[16,128]{1,0:T(8,128)}, u32[]{:S(2)}) copy-start(f32[16,128]{1,0:T(8,128)} %get-tuple-element.6) | copy-start | bytes 24580
  176.5 78.5 %all-to-all-start.2 = ((bf16[8,2,16,5120]{3,2,1,0:T(8,128)(2,1)}), bf16[8,2,16,5120]{3,2,1,0:T(8,128)(2,1)S(1)}, u32[]{:S(2)}, u32[]{:S(2)}) async-start(bf16[8,2,16,5120]{3,2,1,0:T(8,128)(2,1)} %apply.1), calls=%async_computation.2 | async-start | bytes 5242880 | tf_op jit(solution)/shard_map/all_to_all | solution.py:154
